TPU v7x, 256 devices: a 2x2x32 block of a 4x8x32 slice. The times are simulated.
256 devices in a mesh: ens: 4 (over y, x), region: 32 (over z), feat: 2 (over core).
Axes of the slice: x: 2, y: 2, z: 32, core: 2. Of those that a mesh axis runs over, the one named last changes fastest.
The devices are a block of a 4x8x32 slice.
Arguments:
- grid_lat: bfloat16 [131072, 512], P(('ens', 'region', 'feat')), parts along dimension 0, may hold values from -6 to 6
- g2m_edge: bfloat16 [262144, 512], P(('ens', 'region', 'feat')), parts along dimension 0, may hold values from -6 to 6
- g2m_src: int32 [262144], P(('ens', 'region', 'feat')), parts along dimension 0, may hold values from 0 to 32767, as said below
- g2m_owner: int32 [262144, 1], P(('ens', 'region', 'feat')), parts along dimension 0, may hold values from 0 to 63; in each aligned block of 1024 rows (0 to 1023, 1024 to 2047, ...) at most 32 rows name the same one
- g2m_row: int32 [262144], P(('ens', 'region', 'feat')), parts along dimension 0, may hold values from 0 to 255
- mesh_lat: bfloat16 [65536, 512], P(('ens', 'region', 'feat')), parts along dimension 0, may hold values from -6 to 6
- m2m_edge: bfloat16 [65536, 8, 512], P(('ens', 'region', 'feat')), parts along dimension 0, may hold values from -6 to 6
- m2m_src: int32 [65536, 8], P(('ens', 'region', 'feat')), parts along dimension 0, may hold values from 0 to 16383, as said below
- enc_edge_w: bfloat16 [4, 512, 512], P(None, None, 'feat'), may hold values from -0.25 to 0.25
- enc_node_w: bfloat16 [3, 512, 512], P(None, None, 'feat'), may hold values from -0.25 to 0.25
- proc_edge_w: bfloat16 [2, 4, 512, 512], P(None, None, None, 'feat'), may hold values from -0.25 to 0.25
- proc_node_w: bfloat16 [2, 3, 512, 512], P(None, None, None, 'feat'), may hold values from -0.25 to 0.25
Outputs:
- mesh_out: bfloat16 [65536, 512], P(('ens', 'region', 'feat')), parts along dimension 0
There are 4 independent parts, one for each index of `ens`. A program takes and returns all parts, laid end to end along the dimension named above; an argument that names none is the same for every part. Nothing has to cross between parts.
Inputs may be any that keep to these rules, and one draw needn't show every extreme that they name: Edge i is sent by a grid node of block i // 1024, that is g2m_src[i] // 512 == i // 1024. `g2m_owner`: among the 1024 edges of one block, at most 32 have the same owner. `m2m_src`: for a receiving node v of block b = v // 256, every sender s has s % 256 < 8, or b * 256 - 128 <= s < (b + 1) * 256 + 128.
All inputs are finite; a program needn't handle non-finite values.
Results may differ from a plain program's by a relative error of at most 0.017.
Values may be sent and summed in bfloat16 or wider, within the bound.
No kernel may reach another device: no remote copies, remote signals or barrier semaphores. Data moves between devices by JAX's collectives and lax.ppermute only.
A program may use at most 128 MiB of HBM per device.

v0:
```python
import jax
import jax.numpy as jnp
from jax import lax
from jax.sharding import PartitionSpec as P

MC_DEV = 8


def extended(value, sides, width):
    edges = {}
    for axis, dim in sides:
        size, length = (lax.axis_size(axis), value.shape[dim])
        up = [(i, (i + 1) % size) for i in range(size - 1)]
        last = lax.slice_in_dim(value, length - width, length, axis=dim)
        initial = lax.slice_in_dim(value, 0, width, axis=dim)
        edges[dim] = (
            lax.ppermute(last, axis, up),
            lax.ppermute(initial, axis, [(b, a) for a, b in up]),
        )
    done = []
    for _, dim in sides:
        low, high = edges[dim]
        around = [(width, width) if d in done else (0, 0) for d in range(value.ndim)]
        value = jnp.concatenate([jnp.pad(low, around), value, jnp.pad(high, around)], axis=dim)
        done.append(dim)
    return value


def in_order(pieces, dim):
    dims = list(pieces.shape[1:])
    dims[dim] *= pieces.shape[0]
    return jnp.moveaxis(pieces, 0, dim).reshape(dims)


def all_blocks(value, axes, sequence):
    pieces = value
    for k in sequence:
        pieces = lax.all_gather(pieces, axes[k])
    done = sequence[::-1]
    back = [done.index(k) for k in range(len(axes))]
    pieces = pieces.transpose(*back, *range(len(axes), pieces.ndim))
    return pieces.reshape(-1, *value.shape)


def gather_axes(value, axes, sequence, dim):
    return in_order(all_blocks(value, axes, sequence), dim)


def layer_norm(values):
    center = values - jnp.mean(values, axis=-1, keepdims=True)
    spread = jnp.mean(center * center, axis=-1, keepdims=True)
    return center * lax.rsqrt(spread + 1e-05)


def project(latent, matrix):
    return jnp.dot(latent, matrix, preferred_element_type=jnp.float32).astype(jnp.bfloat16)


def edge_output(pre_act, matrix):
    hidden = jax.nn.silu(pre_act).astype(jnp.bfloat16)
    return layer_norm(jnp.dot(hidden, matrix, preferred_element_type=jnp.float32)).astype(
        jnp.bfloat16
    )


def node_update(latent, aggregate, stack):
    pre_act = jnp.dot(latent, stack[0], preferred_element_type=jnp.float32)
    pre_act = pre_act + jnp.dot(aggregate, stack[1], preferred_element_type=jnp.float32)
    hidden = jax.nn.silu(pre_act).astype(jnp.bfloat16)
    update = layer_norm(jnp.dot(hidden, stack[2], preferred_element_type=jnp.float32))
    return (latent.astype(jnp.float32) + update).astype(jnp.bfloat16)


def widen(stack):
    return lax.all_gather(stack, "feat", axis=2, tiled=True)


def on_device(
    grid_lat,
    g2m_edge,
    g2m_src,
    g2m_owner,
    g2m_row,
    mesh_lat,
    m2m_edge,
    m2m_src,
    enc_edge_w,
    enc_node_w,
    proc_edge_w,
    proc_node_w,
):
    shards = lax.axis_size(("region", "feat"))
    myself = lax.axis_index(("region", "feat"))
    grid_rows = grid_lat.shape[0]
    mesh_rows = mesh_lat.shape[0]
    edge_count = g2m_edge.shape[0]
    width = grid_lat.shape[1]
    capacity = 2 * edge_count // shards
    slot_total = shards * capacity
    edge_stack = widen(enc_edge_w)
    sender = project(grid_lat, edge_stack[1])
    receiver = project(mesh_lat, edge_stack[2])
    local_src = g2m_src - myself * grid_rows
    owner = g2m_owner[:, 0]
    onehot = (owner[:, None] == jnp.arange(shards, dtype=jnp.int32)[None, :]).astype(jnp.int32)
    rank = jnp.sum((jnp.cumsum(onehot, axis=0) - 1) * onehot, axis=1)
    slot = owner * capacity + rank
    slot_edge = (
        jnp.zeros((slot_total,), jnp.int32).at[slot].set(jnp.arange(edge_count, dtype=jnp.int32))
    )
    filled = jnp.zeros((slot_total,), jnp.bool_).at[slot].set(True)
    row_slots = jnp.where(filled, g2m_row[slot_edge], -1).reshape(shards, capacity)
    partial_sum = jnp.dot(g2m_edge, edge_stack[0], preferred_element_type=jnp.float32)
    partial_sum = (partial_sum + sender[local_src].astype(jnp.float32)).astype(jnp.bfloat16)
    packed = partial_sum[slot_edge].reshape(shards, capacity, width)
    got_partial, got_targets = (
        lax.all_to_all(packed, ("region", "feat"), split_axis=0, concat_axis=0, tiled=True),
        lax.all_to_all(row_slots, ("region", "feat"), split_axis=0, concat_axis=0, tiled=True),
    )
    targets = got_targets.reshape(slot_total)
    safe = jnp.maximum(targets, 0)
    pre_act = got_partial.reshape(slot_total, width).astype(jnp.float32) + receiver[safe].astype(
        jnp.float32
    )
    message = edge_output(pre_act, edge_stack[3])
    terms = jnp.where((targets >= 0)[:, None], message.astype(jnp.float32), 0.0)
    aggregate = jax.ops.segment_sum(terms, safe, num_segments=mesh_rows)
    mesh = node_update(mesh_lat, aggregate.astype(jnp.bfloat16), widen(enc_node_w))
    kdeg = m2m_src.shape[1]
    halo_rows = mesh_rows // 2
    senders = m2m_src.reshape(mesh_rows * kdeg)
    home = senders // mesh_rows
    inside = senders % mesh_rows
    table_index = jnp.where(
        inside < MC_DEV,
        mesh_rows + 2 * halo_rows + home * MC_DEV + inside,
        senders - (myself * mesh_rows - halo_rows),
    )
    edges = m2m_edge.reshape(mesh_rows * kdeg, width)
    for layer in range(proc_edge_w.shape[0]):
        layer_edge = widen(proc_edge_w[layer])
        layer_node = widen(proc_node_w[layer])
        sender = project(mesh, layer_edge[1])
        receiver = project(mesh, layer_edge[2])
        bordered = extended(sender, ((("region", "feat"), 0),), halo_rows)
        coarse_rows = gather_axes(sender[:MC_DEV], ("region", "feat"), (0, 1), 0)
        table = jnp.concatenate([bordered, coarse_rows], axis=0)
        pre_act = jnp.dot(edges, layer_edge[0], preferred_element_type=jnp.float32)
        pre_act = (
            pre_act
            + table[table_index].astype(jnp.float32)
            + jnp.repeat(receiver, kdeg, axis=0).astype(jnp.float32)
        )
        message = edge_output(pre_act, layer_edge[3])
        aggregate = jnp.sum(message.astype(jnp.float32).reshape(mesh_rows, kdeg, width), axis=1)
        edges = (edges.astype(jnp.float32) + message.astype(jnp.float32)).astype(jnp.bfloat16)
        mesh = node_update(mesh, aggregate.astype(jnp.bfloat16), layer_node)
    return mesh


def solution(mesh):
    return jax.shard_map(
        on_device,
        mesh=mesh,
        in_specs=(
            P(("ens", "region", "feat"), None),
            P(("ens", "region", "feat"), None),
            P(("ens", "region", "feat")),
            P(("ens", "region", "feat"), None),
            P(("ens", "region", "feat")),
            P(("ens", "region", "feat"), None),
            P(("ens", "region", "feat"), None, None),
            P(("ens", "region", "feat"), None),
            P(None, None, "feat"),
            P(None, None, "feat"),
            P(None, None, None, "feat"),
            P(None, None, None, "feat"),
        ),
        out_specs=P(("ens", "region", "feat"), None),
        check_vma=False,
    )
```

profile of v0, /device:TPU:37, one launch (start us, length us, event | category | flops | bytes accessed | tf_op | source)
XLA Modules:
  0.0 537.7 jit_solution(10828979515456356212)
XLA Ops:
  6.6 0.7 all-gather.17.cloned.1.call-update
  7.3 0.7 fusion.39
  8.0 18.0 %reduce-window.6 = s32[64,8,128]{2,1,0:T(8,128)S(1)} reduce-window(s32[64,8,128]{2,1,0:T(8,128)S(1)} %fusion.39, s32[]{:T(128)} %constant.81.clone.1), window={size=1x1x128 pad=0_0x0_0x127_0}, to_apply=%region_0.0 | reduce-window | flops 8323072 | bytes 524292 | tf_op jit(solution)/shard_map/reduce-window
  26.7 4.3 scatter_custom_fusion.1
  31.1 8.6 %gather_fusion = s32[2048]{0:T(1024)S(1)} fusion(s32[1024]{0:T(1024)S(1)} %copy-done.2, s32[2048]{0:T(1024)S(1)} %fusion.40), kind=kCustom, calls=%fused_computation | custom fusion | bytes 24576 | tf_op jit(solution)/shard_map/gather | solution.py:112
  39.7 4.3 scatter_custom_fusion
  44.0 0.7 all_to_all.9
  44.7 34.3 %all-to-all-start = ((s32[64,1,32]{2,1,0:T(1,128)}), s32[64,1,32]{2,1,0:T(1,128)S(1)}, u32[]{:S(2)}, u32[]{:S(2)}) async-start(s32[64,1,32]{2,1,0:T(1,128)} %bitcast.7), calls=%async_computation | async-start | bytes 65536 | tf_op jit(solution)/shard_map/all_to_all | solution.py:118
  79.1 1.5 convolution_convert_fusion
  80.6 4.0 gather_fusion.1
  84.6 1.7 add_convert_fusion
  86.3 9.2 %gather_fusion.2 = bf16[2048,512]{1,0:T(8,128)(2,1)} fusion(bf16[1024,512]{1,0:T(8,128)(2,1)S(1)} %add_convert_fusion, s32[2048]{0:T(1024)S(1)} %fusion.40), kind=kCustom, calls=%fused_computation.2 | custom fusion | bytes 4202496 | tf_op jit(solution)/shard_map/gather | solution.py:115
  95.5 5.5 %all-to-all-done = s32[64,1,32]{2,1,0:T(1,128)S(1)} async-done(((s32[64,1,32]{2,1,0:T(1,128)}), s32[64,1,32]{2,1,0:T(1,128)S(1)}, u32[]{:S(2)}, u32[]{:S(2)}) %all-to-all-start) | async-done | bytes 8224 | tf_op jit(solution)/shard_map/all_to_all | solution.py:118
  101.0 17.9 %all-to-all-start.1 = ((bf16[64,32,512]{2,1,0:T(8,128)(2,1)}), bf16[64,32,512]{2,1,0:T(8,128)(2,1)}, u32[]{:S(2)}, u32[]{:S(2)}) async-start(bf16[64,32,512]{2,1,0:T(8,128)(2,1)} %bitcast.189), calls=%async_computation.1 | async-start | bytes 4194304 | tf_op jit(solution)/shard_map/all_to_all | solution.py:117
  119.0 0.7 all-gather.15.cloned.1.call-update
  119.8 1.5 fusion.51
  121.4 2.6 fusion.52
  124.1 0.2 all-gather.25.cloned.1.call-start
  124.4 0.4 all-gather.25.cloned.1.call-update
  124.8 0.6 all-gather.23.cloned.1.call-update
  126.1 24.3 %all-gather.15.cloned.1.call-done = bf16[3,512,512]{2,1,0:T(8,128)(2,1)} async-done(((bf16[3,512,256]{2,1,0:T(8,128)(2,1)}), bf16[3,512,512]{2,1,0:T(8,128)(2,1)}) %all-gather.15.cloned.1.call-update) | async-done | bytes 1572880 | tf_op jit(solution)/shard_map/all_gather | solution.py:75
  150.5 2.1 fusion.27
  152.6 1.3 convolution_convert_fusion.5
  154.0 7.5 %gather_fusion.3 = bf16[2048,512]{1,0:T(8,128)(2,1)S(1)} fusion(bf16[256,512]{1,0:T(8,128)(2,1)S(1)} %convolution_convert_fusion.5, s32[2048]{0:T(1024)S(1)} %broadcast_clamp_fusion), kind=kCustom, calls=%fused_computation.3 | custom fusion | bytes 4202496 | tf_op jit(solution)/shard_map/gather | solution.py:122
  161.5 154.8 %all-to-all-done.1 = bf16[64,32,512]{2,1,0:T(8,128)(2,1)} async-done(((bf16[64,32,512]{2,1,0:T(8,128)(2,1)}), bf16[64,32,512]{2,1,0:T(8,128)(2,1)}, u32[]{:S(2)}, u32[]{:S(2)}) %all-to-all-start.1) | async-done | bytes 2097184 | tf_op jit(solution)/shard_map/all_to_all | solution.py:117
  316.4 2.8 multiply_convert_fusion.5
  319.1 2.3 fusion.55
  321.5 0.5 multiply_reduce_fusion.2
  322.0 2.5 convert_select_fusion
  324.5 5.4 %copy.24 = f32[2048,512]{1,0:T(8,128)} copy(f32[2048,512]{0,1:T(8,128)} %convert_select_fusion) | data formatting | bytes 8388608 | tf_op jit(solution)/shard_map/jit(_where)/select_n | solution.py:126
  329.9 14.4 %scatter_custom_fusion.2 = f32[256,512]{1,0:T(8,128)S(1)} fusion(s32[2048]{0:T(1024)S(1)} %reshape.348, f32[2048,512]{1,0:T(8,128)} %copy.24, f32[]{:T(128)} %constant.78.clone.1), kind=kCustom, calls=%fused_computation.96 | custom fusion | flops 1048576 | bytes 524800 | tf_op jit(solution)/shard_map/scatter-add | solution.py:127
  344.3 1.9 fusion.56
  346.2 0.2 multiply_reduce_fusion.5
  346.4 0.2 add_convert_fusion.3
  346.6 1.3 convolution_convert_fusion.4
  348.0 38.9 %all-gather.2 = bf16[256,512]{1,0:T(8,128)(2,1)S(1)} all-gather(bf16[8,512]{1,0:T(8,128)(2,1)S(1)} %slice.172), channel_id=4, replica_groups=mesh['ens'=4,'region'=32,'feat'=2] {'region'}, dimensions={0}, use_global_device_ids=true | all-gather | bytes 270336 | tf_op jit(solution)/shard_map/all_gather | solution.py:38
  386.9 18.3 %all-gather.3 = bf16[64,8,512]{2,1,0:T(8,128)(2,1)S(1)} all-gather(bf16[32,8,512]{2,1,0:T(8,128)(2,1)S(1)} %bitcast.194), channel_id=5, replica_groups=mesh['ens'=4,'region'=32,'feat'=2] {'feat'}, dimensions={0}, use_global_device_ids=true | all-gather | bytes 786432 | tf_op jit(solution)/shard_map/all_gather | solution.py:38
  405.2 3.8 collective-permute-start
  409.0 2.2 collective-permute-start.1
  411.2 1.3 fusion.20
  412.6 1.3 fusion.24
  413.9 1.4 collective-permute-done.1
  415.4 9.2 %gather_fusion.4 = bf16[2048,512]{1,0:T(8,128)(2,1)} fusion(bf16[1024,512]{1,0:T(8,128)(2,1)S(1)} %pad_maximum_fusion, s32[2048]{0:T(1024)S(1)} %broadcast_clamp_fusion.1), kind=kCustom, calls=%fused_computation.4 | custom fusion | bytes 4202496 | tf_op jit(solution)/shard_map/gather | solution.py:151
  424.6 7.2 %fusion.59 = (f32[2048]{0:T(1024)S(1)}, f32[2048,512]{1,0:T(8,128)}) fusion(bf16[1,4,512,512]{3,2,1,0:T(8,128)(2,1)} %all-gather.21.cloned.1.call-done, bf16[2048,512]{1,0:T(8,128)(2,1)} %gather_fusion.4, f32[256,512]{1,0:T(8,128)S(1)} %fusion.20, bf16[256,8,512]{2,1,0:T(8,128)(2,1)} %param.18), kind=kOutput, calls=%fused_computation.143 | convolution fusion | flops 2156918784 | bytes 9969664 | tf_op jit(solution)/shard_map/dot_general | solution.py:61
  431.8 3.0 multiply_reduce_fusion.1
  434.9 0.4 copy-done.3
  435.3 2.7 fusion
  438.0 1.9 fusion.62
  439.9 0.2 multiply_reduce_fusion.4
  440.3 1.3 convolution_convert_fusion.2
  441.6 39.1 %all-gather.6 = bf16[256,512]{1,0:T(8,128)(2,1)S(1)} all-gather(bf16[8,512]{1,0:T(8,128)(2,1)S(1)} %slice.182), channel_id=8, replica_groups=mesh['ens'=4,'region'=32,'feat'=2] {'region'}, dimensions={0}, use_global_device_ids=true | all-gather | bytes 270336 | tf_op jit(solution)/shard_map/all_gather | solution.py:38
  480.7 16.0 %all-gather.7 = bf16[64,8,512]{2,1,0:T(8,128)(2,1)S(1)} all-gather(bf16[32,8,512]{2,1,0:T(8,128)(2,1)S(1)} %bitcast.195), channel_id=9, replica_groups=mesh['ens'=4,'region'=32,'feat'=2] {'feat'}, dimensions={0}, use_global_device_ids=true | all-gather | bytes 786432 | tf_op jit(solution)/shard_map/all_gather | solution.py:38
  496.9 2.0 collective-permute-start.2
  498.8 2.7 collective-permute-start.3
  501.5 2.2 fusion.19
  503.7 2.1 fusion.22
  505.9 9.2 %gather_fusion.5 = bf16[2048,512]{1,0:T(8,128)(2,1)} fusion(bf16[1024,512]{1,0:T(8,128)(2,1)S(1)} %pad_maximum_fusion.1, s32[2048]{0:T(1024)S(1)} %broadcast_clamp_fusion.1), kind=kCustom, calls=%fused_computation.5 | custom fusion | bytes 4202496 | tf_op jit(solution)/shard_map/gather | solution.py:151
  515.1 7.5 %fusion.63 = (f32[2048]{0:T(1024)S(1)}, f32[2048,512]{1,0:T(8,128)}) fusion(bf16[1,4,512,512]{3,2,1,0:T(8,128)(2,1)} %all-gather.25.cloned.1.call-done, bf16[2048,512]{1,0:T(8,128)(2,1)} %gather_fusion.5, f32[256,512]{1,0:T(8,128)} %fusion.19, bf16[2048,512]{1,0:T(8,128)(2,1)S(1)} %copy-done.5, bf16[256,8,512]{2,1,0:T(8,128)(2,1)} %param.18), kind=kOutput, calls=%fused_computation.145 | convolution fusion | flops 2161113088 | bytes 12066816 | tf_op jit(solution)/shard_map/dot_general | solution.py:61
  522.7 3.0 multiply_reduce_fusion
  525.7 0.4 copy-done.4
  526.1 1.8 fusion.3
  527.9 1.9 fusion.66
  529.8 0.2 multiply_reduce_fusion.3
  530.0 0.9 add_convert_fusion.1
  (84 shorter events, 2.3 us)
Async XLA Ops:
  6.5 78.0 %copy-start = (bf16[1024,512]{1,0:T(8,128)(2,1)S(1)}, bf16[1024,512]{1,0:T(8,128)(2,1)}, u32[]{:S(2)}) copy-start(bf16[1024,512]{1,0:T(8,128)(2,1)} %param.13) | copy-start | bytes 3145732
  6.6 20.0 %copy-start.10 = (s32[1024,1]{0,1:T(1,128)S(1)}, s32[1024,1]{0,1:T(1,128)}, u32[]{:S(2)}) copy-start(s32[1024,1]{0,1:T(1,128)} %param.15) | copy-start | bytes 12292
  6.6 24.5 %copy-start.2 = (s32[1024]{0:T(1024)S(1)}, s32[1024]{0:T(1024)}, u32[]{:S(2)}) copy-start(s32[1024]{0:T(1024)} %param.16) | copy-start | bytes 12292
  6.6 72.6 %all-gather.17.cloned.1.call-start = ((), (), s32[]{:S(2)}) async-start(), calls=%async_computation.3 | async-start | bytes 3145728 | tf_op jit(solution)/shard_map/all_gather | solution.py:75
  31.0 48.0 %copy-start.12 = (s32[1024]{0:T(1024)S(1)}, s32[1024]{0:T(1024)}, u32[]{:S(2)}) copy-start(s32[1024]{0:T(1024)} %param.14) | copy-start | bytes 12292
  31.1 48.1 %copy-start.13 = (bf16[512,512]{1,0:T(8,128)(2,1)S(1)}, bf16[512,512]{1,0:T(8,128)(2,1)}, u32[]{:S(2)}) copy-start(bf16[512,512]{1,0:T(8,128)(2,1)} %param.12) | copy-start | bytes 1572868
  44.7 56.3 %all-to-all-start = ((s32[64,1,32]{2,1,0:T(1,128)}), s32[64,1,32]{2,1,0:T(1,128)S(1)}, u32[]{:S(2)}, u32[]{:S(2)}) async-start(s32[64,1,32]{2,1,0:T(1,128)} %bitcast.7), calls=%async_computation | async-start | bytes 65536 | tf_op jit(solution)/shard_map/all_to_all | solution.py:118
  101.0 18.8 %copy-start.6 = (bf16[2,4,512,256]{3,2,1,0:T(8,128)(2,1)S(1)}, bf16[2,4,512,256]{3,2,1,0:T(8,128)(2,1)}, u32[]{:S(2)}) copy-start(bf16[2,4,512,256]{3,2,1,0:T(8,128)(2,1)} %param.22) | copy-start | bytes 6291460
  101.0 215.4 %all-to-all-start.1 = ((bf16[64,32,512]{2,1,0:T(8,128)(2,1)}), bf16[64,32,512]{2,1,0:T(8,128)(2,1)}, u32[]{:S(2)}, u32[]{:S(2)}) async-start(bf16[64,32,512]{2,1,0:T(8,128)(2,1)} %bitcast.189), calls=%async_computation.1 | async-start | bytes 4194304 | tf_op jit(solution)/shard_map/all_to_all | solution.py:117
  118.9 31.6 %all-gather.15.cloned.1.call-start = ((), (), s32[]{:S(2)}) async-start(), calls=%async_computation.2 | async-start | bytes 2359296 | tf_op jit(solution)/shard_map/all_gather | solution.py:75
  119.7 226.9 %all-gather.21.cloned.1.call-start = ((), (), s32[]{:S(2)}) async-start(), calls=%async_computation.5 | async-start | bytes 3145728 | tf_op jit(solution)/shard_map/all_gather | solution.py:75
  121.4 291.2 %all-gather.19.cloned.1.call-start = ((), (), s32[]{:S(2)}) async-start(), calls=%async_computation.4 | async-start | bytes 2359296 | tf_op jit(solution)/shard_map/all_gather | solution.py:75
  124.0 1.4 copy-start.11
  124.0 26.4 %copy-start.7 = (bf16[256,512]{1,0:T(8,128)(2,1)S(1)}, bf16[256,512]{1,0:T(8,128)(2,1)}, u32[]{:S(2)}) copy-start(bf16[256,512]{1,0:T(8,128)(2,1)} %param.17) | copy-start | bytes 786436
  124.1 316.1 %all-gather.25.cloned.1.call-start = ((), (), s32[]{:S(2)}) async-start(), calls=%async_computation.7 | async-start | bytes 3145728 | tf_op jit(solution)/shard_map/all_gather | solution.py:75
  124.8 378.9 %all-gather.23.cloned.1.call-start = ((), (), s32[]{:S(2)}) async-start(), calls=%async_computation.6 | async-start | bytes 2359296 | tf_op jit(solution)/shard_map/all_gather | solution.py:75
  324.5 19.8 %copy-start.8 = (f32[256,512]{1,0:T(8,128)S(1)}, f32[256,512]{1,0:T(8,128)}, u32[]{:S(2)}) copy-start(f32[256,512]{1,0:T(8,128)} %fusion.27) | copy-start | bytes 1572868
  405.2 8.7 %collective-permute-start = (bf16[128,512]{1,0:T(8,128)(2,1)S(1)}, bf16[128,512]{1,0:T(8,128)(2,1)S(1)}, u32[]{:S(2)}, u32[]{:S(2)}) collective-permute-start(bf16[128,512]{1,0:T(8,128)(2,1)S(1)} %get-tuple-element.13), channel_id=1, source_target_pairs={{0,1},{1,2},{2,3},{3,4},{4,5},{5,6},{6,7},{7,8},{8,9},{9,10},{10,1... | collective-permute-start | bytes 393224 | tf_op jit(solution)/shard_map/ppermute | solution.py:17
  409.0 6.3 %collective-permute-start.1 = (bf16[128,512]{1,0:T(8,128)(2,1)S(1)}, bf16[128,512]{1,0:T(8,128)(2,1)S(1)}, u32[]{:S(2)}, u32[]{:S(2)}) collective-permute-start(bf16[128,512]{1,0:T(8,128)(2,1)S(1)} %get-tuple-element.14), channel_id=1, source_target_pairs={{1,0},{2,1},{3,2},{4,3},{5,4},{6,5},{7,6},{8,7},{9,8},{10,9},{11,1... | collective-permute-start | bytes 393224 | tf_op jit(solution)/shard_map/ppermute | solution.py:18
  431.8 3.4 copy-start.3
  496.9 9.0 %collective-permute-start.2 = (bf16[128,512]{1,0:T(8,128)(2,1)S(1)}, bf16[128,512]{1,0:T(8,128)(2,1)S(1)}, u32[]{:S(2)}, u32[]{:S(2)}) collective-permute-start(bf16[128,512]{1,0:T(8,128)(2,1)S(1)} %get-tuple-element.11), channel_id=1, source_target_pairs={{0,1},{1,2},{2,3},{3,4},{4,5},{5,6},{6,7},{7,8},{8,9},{9,10},{10,1... | collective-permute-start | bytes 393224 | tf_op jit(solution)/shard_map/ppermute | solution.py:17
  498.8 7.0 %collective-permute-start.3 = (bf16[128,512]{1,0:T(8,128)(2,1)S(1)}, bf16[128,512]{1,0:T(8,128)(2,1)S(1)}, u32[]{:S(2)}, u32[]{:S(2)}) collective-permute-start(bf16[128,512]{1,0:T(8,128)(2,1)S(1)} %get-tuple-element.12), channel_id=1, source_target_pairs={{1,0},{2,1},{3,2},{4,3},{5,4},{6,5},{7,6},{8,7},{9,8},{10,9},{11,1... | collective-permute-start | bytes 393224 | tf_op jit(solution)/shard_map/ppermute | solution.py:18
  505.9 9.2 %copy-start.5 = (bf16[2048,512]{1,0:T(8,128)(2,1)S(1)}, bf16[2048,512]{1,0:T(8,128)(2,1)}, u32[]{:S(2)}) copy-start(bf16[2048,512]{1,0:T(8,128)(2,1)} %get-tuple-element.6) | copy-start | bytes 6291460
  522.7 3.4 copy-start.4
  526.1 1.8 copy-start.9
  526.1 4.7 copy-start.1
Sparse Core Ops, SparseCore 0:
  9.2 40.6 all-gather.16
  121.6 28.8 all-gather.14
  152.3 28.3 all-gather.20
  182.4 27.6 all-gather.18
  211.8 28.3 all-gather.24
  241.9 27.6 all-gather.22
where the time goes:
time: 539 us; the launch traced here: 538 us
  waiting for transfers between devices  189 us (35%)
  blocking collectives  112 us (21%)
  local copies, waits for them, and re-layouts  68.2 us (13%)
  starting transfers between devices  63.4 us (12%)
  other arithmetic  52 us (10%)
  matrix products  39 us (7%)
  between operations  14.1 us (3%)
    all_to_all x1, waiting for transfers between devices, on_device(): lax.all_to_all(packed, ('region', 'feat'), split_axis=0, concat_axis=0, t...  155 us
    all_gather x4, blocking collectives, all_blocks(): pieces = lax.all_gather(pieces, axes[k])  112 us
    all_to_all x1, starting transfers between devices, on_device(): lax.all_to_all(row_slots, ('region', 'feat'), split_axis=0, concat_axis=0...  34.3 us
    all_gather x6, waiting for transfers between devices, widen(): return lax.all_gather(stack, 'feat', axis=2, tiled=True)  24.4 us
    gather x2, local copies, waits for them, and re-layouts, on_device(): table[table_index].astype(jnp.float32)  18.4 us
    another operation x2, other arithmetic  18 us
    all_to_all x1, starting transfers between devices, on_device(): lax.all_to_all(packed, ('region', 'feat'), split_axis=0, concat_axis=0, t...  17.9 us
    dot_general x3, matrix products, edge_output(): jnp.dot(hidden, matrix, preferred_element_type=jnp.float32)  17.1 us
  transfers between devices with their start and end apart: 12, of which 4 were waited for; matrix products, arithmetic and copies ran while one was open for 25% of the time, Pallas kernels for 0%

commit v1 on v0

--- a/solution.py
+++ b/solution.py
@@ -72,7 +72,10 @@
 
 
 def widen(stack):
-    return lax.all_gather(stack, "feat", axis=2, tiled=True)
+    return jnp.concatenate(
+        lax.all_to_all(jnp.stack([stack for _ in range(lax.axis_size("feat"))]), "feat", 0, 0),
+        axis=2,
+    )
 
 
 def on_device(

time: 539 us -> 608 us (1.13); the launches traced: 538 us -> 598 us
  local copies, waits for them, and re-layouts: 68.2 us -> 111 us
  blocking collectives: 112 us -> 138 us
  between operations: 14.1 us -> 1.08 us
  other arithmetic: 52 us -> 63.3 us
  matrix products: 39 us -> 31.2 us
    all_to_all x0 -> x2, starting transfers between devices: none -> 28.8 us  [widen(): lax.all_to_all(jnp.stack([stack for _ in range(lax.axis_size('feat'))]),...]
    all_to_all x0 -> x4, blocking collectives: none -> 24.7 us  [widen(): lax.all_to_all(jnp.stack([stack for _ in range(lax.axis_size('feat'))]),...]
    all_gather x6 -> x0, waiting for transfers between devices: 24.4 us -> none  [widen(): return lax.all_gather(stack, 'feat', axis=2, tiled=True)]
    all_to_all x1, waiting for transfers between devices: 155 us -> 176 us  [on_device(): lax.all_to_all(packed, ('region', 'feat'), split_axis=0, concat_axis=0, t...]
    all_to_all x1, starting transfers between devices: 34.3 us -> 14.3 us  [on_device(): lax.all_to_all(row_slots, ('region', 'feat'), split_axis=0, concat_axis=0...]
    convert_element_type x0 -> x7, local copies, waits for them, and re-layouts: none -> 17.8 us  [the longest x4 16 us: on_device(): jnp.repeat(receiver, kdeg, axis=0).astype(jnp.float32)]
    unnamed x29 -> x85, local copies, waits for them, and re-layouts: 0.94 us -> 12.8 us
    another operation x2 -> x8, other arithmetic: 18 us -> 29.3 us
  transfers between devices with their start and end apart: 12 -> 8, of which waited for: 4 -> 2; matrix products, arithmetic and copies ran while one was open for 25% -> 19% of each run, Pallas kernels for 0% -> 0%
where the time goes in v1:
time: 608 us; the launch traced here: 598 us
  waiting for transfers between devices  184 us (30%)
  blocking collectives  138 us (23%)
  local copies, waits for them, and re-layouts  111 us (18%)
  starting transfers between devices  68.9 us (11%)
  other arithmetic  63.3 us (10%)
  matrix products  31.2 us (5%)
    all_to_all x1, waiting for transfers between devices, on_device(): lax.all_to_all(packed, ('region', 'feat'), split_axis=0, concat_axis=0, t...  176 us
    all_gather x4, blocking collectives, all_blocks(): pieces = lax.all_gather(pieces, axes[k])  114 us
    all_to_all x2, starting transfers between devices, widen(): lax.all_to_all(jnp.stack([stack for _ in range(lax.axis_size('feat'))]),...  28.8 us
    all_to_all x4, blocking collectives, widen(): lax.all_to_all(jnp.stack([stack for _ in range(lax.axis_size('feat'))]),...  24.7 us
    gather x4, local copies, waits for them, and re-layouts, on_device(): table[table_index].astype(jnp.float32)  20.1 us
    dot_general x3, matrix products, edge_output(): jnp.dot(hidden, matrix, preferred_element_type=jnp.float32)  18.5 us
    another operation x2, other arithmetic  18 us
    convert_element_type x4, local copies, waits for them, and re-layouts, on_device(): jnp.repeat(receiver, kdeg, axis=0).astype(jnp.float32)  16 us
  transfers between devices with their start and end apart: 8, of which 2 were waited for; matrix products, arithmetic and copies ran while one was open for 19% of the time, Pallas kernels for 0%

profile of v1, /device:TPU:37, one launch (start us, length us, event | category | flops | bytes accessed | tf_op | source)
XLA Modules:
  0.0 597.9 jit_solution(13937337593221986939)
XLA Ops:
  0.0 1.6 copy.60
  1.6 1.5 pad_maximum_fusion
  3.1 24.2 %all-to-all-start.2 = ((bf16[2,4,512,256]{2,3,1,0:T(8,128)(2,1)}), bf16[2,4,512,256]{2,3,1,0:T(8,128)(2,1)S(1)}, u32[]{:S(2)}, u32[]{:S(2)}) async-start(bf16[2,4,512,256]{2,3,1,0:T(8,128)(2,1)} %pad_maximum_fusion), calls=%async_computation.2 | async-start | bytes 4194304 | tf_op jit(solution)/shard_map/all_to_all | solution.py:76
  27.3 2.3 copy.55
  29.6 2.7 pad_maximum_fusion.3
  32.3 4.6 all-to-all-start
  39.2 4.0 gather_fusion.1
  43.2 1.3 copy.63
  44.5 18.0 %reduce-window.6 = s32[64,8,128]{2,1,0:T(8,128)S(1)} reduce-window(s32[64,8,128]{2,1,0:T(8,128)S(1)} %fusion.40, s32[]{:T(128)} %constant.81.clone.1), window={size=1x1x128 pad=0_0x0_0x127_0}, to_apply=%region_0.0 | reduce-window | flops 8323072 | bytes 524292 | tf_op jit(solution)/shard_map/reduce-window
  63.1 4.3 scatter_custom_fusion.1
  67.5 8.6 %gather_fusion = s32[2048]{0:T(1024)S(1)} fusion(s32[1024]{0:T(1024)S(1)} %copy-done.2, s32[2048]{0:T(1024)S(1)} %fusion.41), kind=kCustom, calls=%fused_computation | custom fusion | bytes 24576 | tf_op jit(solution)/shard_map/gather | solution.py:115
  76.1 4.3 scatter_custom_fusion
  81.2 2.8 fusion.53
  83.9 1.5 copy.95
  85.4 1.5 pad_maximum_fusion.1
  89.6 2.8 pad_maximum_fusion.4
  93.0 1.5 pad_maximum_fusion.2
  94.7 1.3 pad_maximum_fusion.5
  96.0 6.4 %all_to_all.44 = bf16[2,4,512,256]{2,3,1,0:T(8,128)(2,1)S(1)} all-to-all(bf16[2,4,512,256]{2,3,1,0:T(8,128)(2,1)} %pad_maximum_fusion.1), channel_id=1, replica_groups=mesh['ens'=4,'region'=32,'feat'=2] {'feat'}, dimensions={0} | all-to-all | bytes 4194304 | tf_op jit(solution)/shard_map/all_to_all | solution.py:76
  102.5 6.0 %all_to_all.45 = bf16[2,3,512,256]{2,3,1,0:T(8,128)(2,1)} all-to-all(bf16[2,3,512,256]{2,3,1,0:T(8,128)(2,1)S(1)} %copy-done.11), channel_id=1, replica_groups=mesh['ens'=4,'region'=32,'feat'=2] {'feat'}, dimensions={0} | all-to-all | bytes 3145728 | tf_op jit(solution)/shard_map/all_to_all | solution.py:76
  108.5 6.4 %all_to_all.46 = bf16[2,4,512,256]{2,3,1,0:T(8,128)(2,1)} all-to-all(bf16[2,4,512,256]{2,3,1,0:T(8,128)(2,1)S(1)} %copy-done.6), channel_id=1, replica_groups=mesh['ens'=4,'region'=32,'feat'=2] {'feat'}, dimensions={0} | all-to-all | bytes 4194304 | tf_op jit(solution)/shard_map/all_to_all | solution.py:76
  115.0 5.8 all_to_all.47
  120.8 14.3 %all-to-all-start.1 = ((s32[64,1,32]{2,1,0:T(1,128)}), s32[64,1,32]{2,1,0:T(1,128)S(1)}, u32[]{:S(2)}, u32[]{:S(2)}) async-start(s32[64,1,32]{2,1,0:T(1,128)} %bitcast.10), calls=%async_computation.1 | async-start | bytes 65536 | tf_op jit(solution)/shard_map/all_to_all | solution.py:121
  135.1 3.1 fusion.10
  138.2 1.5 copy.64
  139.7 9.2 %gather_fusion.2 = bf16[2048,512]{1,0:T(8,128)(2,1)} fusion(bf16[1024,512]{1,0:T(8,128)(2,1)S(1)} %copy.64, s32[2048]{0:T(1024)S(1)} %fusion.41), kind=kCustom, calls=%fused_computation.2 | custom fusion | bytes 4202496 | tf_op jit(solution)/shard_map/gather | solution.py:118
  148.9 8.2 %all-to-all-done.1 = s32[64,1,32]{2,1,0:T(1,128)S(1)} async-done(((s32[64,1,32]{2,1,0:T(1,128)}), s32[64,1,32]{2,1,0:T(1,128)S(1)}, u32[]{:S(2)}, u32[]{:S(2)}) %all-to-all-start.1) | async-done | bytes 8224 | tf_op jit(solution)/shard_map/all_to_all | solution.py:121
  157.1 15.3 %all-to-all-start.3 = ((bf16[64,32,512]{2,1,0:T(8,128)(2,1)}), bf16[64,32,512]{2,1,0:T(8,128)(2,1)}, u32[]{:S(2)}, u32[]{:S(2)}) async-start(bf16[64,32,512]{2,1,0:T(8,128)(2,1)} %bitcast.17), calls=%async_computation.3 | async-start | bytes 4194304 | tf_op jit(solution)/shard_map/all_to_all | solution.py:120
  173.1 1.6 copy.111
  176.3 1.4 copy-done.5
  177.8 1.3 copy-done.10
  182.9 1.4 fusion.54
  184.3 1.4 fusion.52
  186.1 7.5 %gather_fusion.3 = bf16[2048,512]{1,0:T(8,128)(2,1)S(1)} fusion(bf16[256,512]{1,0:T(8,128)(2,1)S(1)} %copy.65, s32[2048]{0:T(1024)S(1)} %broadcast_clamp_fusion), kind=kCustom, calls=%fused_computation.3 | custom fusion | bytes 4202496 | tf_op jit(solution)/shard_map/gather | solution.py:125
  193.6 176.2 %all-to-all-done.3 = bf16[64,32,512]{2,1,0:T(8,128)(2,1)} async-done(((bf16[64,32,512]{2,1,0:T(8,128)(2,1)}), bf16[64,32,512]{2,1,0:T(8,128)(2,1)}, u32[]{:S(2)}, u32[]{:S(2)}) %all-to-all-start.3) | async-done | bytes 2097184 | tf_op jit(solution)/shard_map/all_to_all | solution.py:120
  369.8 2.8 multiply_convert_fusion.5
  372.6 1.3 fusion.62
  374.5 2.5 convert_select_fusion
  377.0 5.4 copy.66
  382.3 14.4 %scatter_custom_fusion.2 = f32[256,512]{1,0:T(8,128)S(1)} fusion(s32[2048]{0:T(1024)S(1)} %reshape.420, f32[2048,512]{1,0:T(8,128)} %copy.66, f32[]{:T(128)} %constant.78.clone.1), kind=kCustom, calls=%fused_computation.90 | custom fusion | flops 1048576 | bytes 524800 | tf_op jit(solution)/shard_map/scatter-add | solution.py:130
  397.1 2.0 fusion.63
  399.9 38.9 %all-gather = bf16[256,512]{1,0:T(8,128)(2,1)S(1)} all-gather(bf16[8,512]{1,0:T(8,128)(2,1)S(1)} %slice.179), channel_id=2, replica_groups=mesh['ens'=4,'region'=32,'feat'=2] {'region'}, dimensions={0}, use_global_device_ids=true | all-gather | bytes 270336 | tf_op jit(solution)/shard_map/all_gather | solution.py:38
  438.8 18.3 %all-gather.1 = bf16[64,8,512]{2,1,0:T(8,128)(2,1)S(1)} all-gather(bf16[32,8,512]{2,1,0:T(8,128)(2,1)S(1)} %bitcast.191), channel_id=3, replica_groups=mesh['ens'=4,'region'=32,'feat'=2] {'feat'}, dimensions={0}, use_global_device_ids=true | all-gather | bytes 786432 | tf_op jit(solution)/shard_map/all_gather | solution.py:38
  457.2 3.8 collective-permute-start
  461.0 2.1 collective-permute-start.1
  463.4 2.5 broadcast_bitcast_fusion.1
  466.0 5.5 copy.75
  472.7 7.5 %gather_fusion.4 = bf16[2048,512]{1,0:T(8,128)(2,1)S(1)} fusion(bf16[1024,512]{1,0:T(8,128)(2,1)S(1)} %pad_maximum_fusion.6, s32[2048]{0:T(1024)S(1)} %broadcast_clamp_fusion.1), kind=kCustom, calls=%fused_computation.4 | custom fusion | bytes 4202496 | tf_op jit(solution)/shard_map/gather | solution.py:154
  480.2 2.5 copy.74
  482.7 8.2 %fusion.64 = (f32[2048]{0:T(1024)S(1)}, f32[2048,512]{1,0:T(8,128)}) fusion(bf16[512,512]{0,1:T(8,128)(2,1)S(1)} %bitcast.203, f32[2048,512]{0,1:T(8,128)} %copy.75, bf16[2048,512]{0,1:T(8,128)(2,1)} %copy.74, bf16[512,512]{0,1:T(8,128)(2,1)S(1)} %bitcast.202, bf16[256,8,512]{2,1,0:T(8,128)(2,1)} %param.18), kind=kOutput, calls=%fused_computation.143 | convolution fusion | flops 2156918784 | bytes 13639680 | tf_op jit(solution)/shard_map/dot_general | solution.py:61
  491.0 3.0 multiply_reduce_fusion.1
  494.4 2.6 fusion
  498.8 39.1 %all-gather.2 = bf16[256,512]{1,0:T(8,128)(2,1)S(1)} all-gather(bf16[8,512]{1,0:T(8,128)(2,1)S(1)} %slice.189), channel_id=4, replica_groups=mesh['ens'=4,'region'=32,'feat'=2] {'region'}, dimensions={0}, use_global_device_ids=true | all-gather | bytes 270336 | tf_op jit(solution)/shard_map/all_gather | solution.py:38
  537.9 17.4 %all-gather.3 = bf16[64,8,512]{2,1,0:T(8,128)(2,1)S(1)} all-gather(bf16[32,8,512]{2,1,0:T(8,128)(2,1)S(1)} %bitcast.192), channel_id=5, replica_groups=mesh['ens'=4,'region'=32,'feat'=2] {'feat'}, dimensions={0}, use_global_device_ids=true | all-gather | bytes 786432 | tf_op jit(solution)/shard_map/all_gather | solution.py:38
  555.4 2.0 collective-permute-start.2
  557.4 2.7 collective-permute-start.3
  560.4 2.5 broadcast_bitcast_fusion
  562.9 5.5 copy.85
  569.6 7.5 %gather_fusion.5 = bf16[2048,512]{1,0:T(8,128)(2,1)S(1)} fusion(bf16[1024,512]{1,0:T(8,128)(2,1)S(1)} %pad_maximum_fusion.7, s32[2048]{0:T(1024)S(1)} %broadcast_clamp_fusion.1), kind=kCustom, calls=%fused_computation.5 | custom fusion | bytes 4202496 | tf_op jit(solution)/shard_map/gather | solution.py:154
  577.2 2.5 copy.83
  579.6 9.0 %fusion.68 = (f32[2048]{0:T(1024)S(1)}, f32[2048,512]{1,0:T(8,128)}) fusion(bf16[512,512]{0,1:T(8,128)(2,1)S(1)} %bitcast.201, f32[2048,512]{0,1:T(8,128)} %copy.85, bf16[2048,512]{0,1:T(8,128)(2,1)} %copy.83, bf16[512,512]{0,1:T(8,128)(2,1)S(1)} %bitcast.200, bf16[2048,512]{1,0:T(8,128)(2,1)} %get-tuple-element.6, bf16[256,8,512]{2,1,0:T(8,128)(2,1)} %param.18), kind=kOutput, calls=%fused_computation.145 | convolution fusion | flops 2161113088 | bytes 15736832 | tf_op jit(solution)/shard_map/dot_general | solution.py:61
  588.7 3.0 multiply_reduce_fusion
  592.1 2.5 fusion.4
  594.6 1.9 fusion.71
  (158 shorter events, 22.0 us)
Async XLA Ops:
  0.0 135.1 %copy-start = (bf16[1024,512]{1,0:T(8,128)(2,1)S(1)}, bf16[1024,512]{1,0:T(8,128)(2,1)}, u32[]{:S(2)}) copy-start(bf16[1024,512]{1,0:T(8,128)(2,1)} %param.13) | copy-start | bytes 3145732
  3.1 29.2 %all-to-all-start.2 = ((bf16[2,4,512,256]{2,3,1,0:T(8,128)(2,1)}), bf16[2,4,512,256]{2,3,1,0:T(8,128)(2,1)S(1)}, u32[]{:S(2)}, u32[]{:S(2)}) async-start(bf16[2,4,512,256]{2,3,1,0:T(8,128)(2,1)} %pad_maximum_fusion), calls=%async_computation.2 | async-start | bytes 4194304 | tf_op jit(solution)/shard_map/all_to_all | solution.py:76
  32.3 63.7 %all-to-all-start = ((bf16[2,3,512,256]{2,3,1,0:T(8,128)(2,1)}), bf16[2,3,512,256]{2,3,1,0:T(8,128)(2,1)}, u32[]{:S(2)}, u32[]{:S(2)}) async-start(bf16[2,3,512,256]{2,3,1,0:T(8,128)(2,1)} %pad_maximum_fusion.3), calls=%async_computation | async-start | bytes 3145728 | tf_op jit(solution)/shard_map/all_to_all | solution.py:76
  37.2 1.3 copy-start.24
  38.4 0.7 copy-start.38
  43.1 1.3 copy-start.36
  43.1 24.3 %copy-start.2 = (s32[1024]{0:T(1024)S(1)}, s32[1024]{0:T(1024)}, u32[]{:S(2)}) copy-start(s32[1024]{0:T(1024)} %param.16) | copy-start | bytes 12292
  85.4 2.1 copy-start.22
  92.9 1.5 copy-start.13
  96.0 6.4 %copy-start.11 = (bf16[2,3,512,256]{2,3,1,0:T(8,128)(2,1)S(1)}, bf16[2,3,512,256]{2,3,1,0:T(8,128)(2,1)}, u32[]{:S(2)}) copy-start(bf16[2,3,512,256]{2,3,1,0:T(8,128)(2,1)} %pad_maximum_fusion.4) | copy-start | bytes 4718596
  102.5 6.0 %copy-start.6 = (bf16[2,4,512,256]{2,3,1,0:T(8,128)(2,1)S(1)}, bf16[2,4,512,256]{2,3,1,0:T(8,128)(2,1)}, u32[]{:S(2)}) copy-start(bf16[2,4,512,256]{2,3,1,0:T(8,128)(2,1)} %pad_maximum_fusion.2) | copy-start | bytes 6291460
  108.5 6.4 %copy-start.12 = (bf16[2,3,512,256]{2,3,1,0:T(8,128)(2,1)S(1)}, bf16[2,3,512,256]{2,3,1,0:T(8,128)(2,1)}, u32[]{:S(2)}) copy-start(bf16[2,3,512,256]{2,3,1,0:T(8,128)(2,1)} %pad_maximum_fusion.5) | copy-start | bytes 4718596
  120.8 36.3 %all-to-all-start.1 = ((s32[64,1,32]{2,1,0:T(1,128)}), s32[64,1,32]{2,1,0:T(1,128)S(1)}, u32[]{:S(2)}, u32[]{:S(2)}) async-start(s32[64,1,32]{2,1,0:T(1,128)} %bitcast.10), calls=%async_computation.1 | async-start | bytes 65536 | tf_op jit(solution)/shard_map/all_to_all | solution.py:121
  157.0 15.3 %copy-start.19 = (bf16[1,512,2,256]{1,3,2,0:T(8,128)(2,1)S(1)}, bf16[1,512,2,256]{1,3,2,0:T(8,128)(2,1)}, u32[]{:S(2)}) copy-start(bf16[1,512,2,256]{1,3,2,0:T(8,128)(2,1)} %get-tuple-element.18) | copy-start | bytes 1572868
  157.1 15.3 %copy-start.23 = (bf16[256,512]{1,0:T(8,128)(2,1)S(1)}, bf16[256,512]{1,0:T(8,128)(2,1)}, u32[]{:S(2)}) copy-start(bf16[256,512]{1,0:T(8,128)(2,1)} %param.17) | copy-start | bytes 786436
  157.1 15.8 %copy-start.37 = (s32[256,8]{0,1:T(8,128)S(1)}, s32[256,8]{0,1:T(8,128)}, u32[]{:S(2)}) copy-start(s32[256,8]{0,1:T(8,128)} %param.19) | copy-start | bytes 24580
  157.1 212.7 %all-to-all-start.3 = ((bf16[64,32,512]{2,1,0:T(8,128)(2,1)}), bf16[64,32,512]{2,1,0:T(8,128)(2,1)}, u32[]{:S(2)}, u32[]{:S(2)}) async-start(bf16[64,32,512]{2,1,0:T(8,128)(2,1)} %bitcast.17), calls=%async_computation.3 | async-start | bytes 4194304 | tf_op jit(solution)/shard_map/all_to_all | solution.py:120
  174.7 1.4 copy-start.9
  176.1 1.6 copy-start.5
  177.7 1.4 copy-start.10
  369.8 2.8 copy-start.16
  382.3 14.8 %copy-start.31 = (bf16[1,512,2,256]{1,3,2,0:T(8,128)(2,1)S(1)}, bf16[1,512,2,256]{1,3,2,0:T(8,128)(2,1)}, u32[]{:S(2)}) copy-start(bf16[1,512,2,256]{1,3,2,0:T(8,128)(2,1)} %get-tuple-element.29) | copy-start | bytes 1572868
  397.1 2.4 copy-start.21
  399.5 71.9 %copy-start.7 = (bf16[256,512]{1,0:T(8,128)(2,1)}, bf16[256,512]{1,0:T(8,128)(2,1)S(1)}, u32[]{:S(2)}) copy-start(bf16[256,512]{1,0:T(8,128)(2,1)S(1)} %add_convert_fusion.2) | copy-start | bytes 786436
  399.5 63.6 %copy-start.20 = (bf16[1,512,2,256]{1,3,2,0:T(8,128)(2,1)S(1)}, bf16[1,512,2,256]{1,3,2,0:T(8,128)(2,1)}, u32[]{:S(2)}) copy-start(bf16[1,512,2,256]{1,3,2,0:T(8,128)(2,1)} %get-tuple-element.15) | copy-start | bytes 1572868
  457.2 15.4 %collective-permute-start = (bf16[128,512]{1,0:T(8,128)(2,1)S(1)}, bf16[128,512]{1,0:T(8,128)(2,1)S(1)}, u32[]{:S(2)}, u32[]{:S(2)}) collective-permute-start(bf16[128,512]{1,0:T(8,128)(2,1)S(1)} %get-tuple-element.34), channel_id=1, source_target_pairs={{0,1},{1,2},{2,3},{3,4},{4,5},{5,6},{6,7},{7,8},{8,9},{9,10},{10,1... | collective-permute-start | bytes 393224 | tf_op jit(solution)/shard_map/ppermute | solution.py:17
  461.0 11.6 %collective-permute-start.1 = (bf16[128,512]{1,0:T(8,128)(2,1)S(1)}, bf16[128,512]{1,0:T(8,128)(2,1)S(1)}, u32[]{:S(2)}, u32[]{:S(2)}) collective-permute-start(bf16[128,512]{1,0:T(8,128)(2,1)S(1)} %get-tuple-element.35), channel_id=1, source_target_pairs={{1,0},{2,1},{3,2},{4,3},{5,4},{6,5},{7,6},{8,7},{9,8},{10,9},{11,1... | collective-permute-start | bytes 393224 | tf_op jit(solution)/shard_map/ppermute | solution.py:18
  466.0 5.5 copy-start.15
  480.2 2.5 copy-start.34
  480.2 2.5 copy-start.35
  491.0 3.4 copy-start.3
  494.4 2.6 copy-start.26
  494.4 2.6 copy-start.29
  494.4 2.7 copy-start.30
  497.1 1.2 copy-start.8
  497.1 1.3 copy-start.18
  498.4 61.6 %copy-start.17 = (bf16[1,512,2,256]{1,3,2,0:T(8,128)(2,1)S(1)}, bf16[1,512,2,256]{1,3,2,0:T(8,128)(2,1)}, u32[]{:S(2)}) copy-start(bf16[1,512,2,256]{1,3,2,0:T(8,128)(2,1)} %get-tuple-element.9) | copy-start | bytes 1572868
  555.4 14.1 %collective-permute-start.2 = (bf16[128,512]{1,0:T(8,128)(2,1)S(1)}, bf16[128,512]{1,0:T(8,128)(2,1)S(1)}, u32[]{:S(2)}, u32[]{:S(2)}) collective-permute-start(bf16[128,512]{1,0:T(8,128)(2,1)S(1)} %get-tuple-element.32), channel_id=1, source_target_pairs={{0,1},{1,2},{2,3},{3,4},{4,5},{5,6},{6,7},{7,8},{8,9},{9,10},{10,1... | collective-permute-start | bytes 393224 | tf_op jit(solution)/shard_map/ppermute | solution.py:17
  557.4 12.2 %collective-permute-start.3 = (bf16[128,512]{1,0:T(8,128)(2,1)S(1)}, bf16[128,512]{1,0:T(8,128)(2,1)S(1)}, u32[]{:S(2)}, u32[]{:S(2)}) collective-permute-start(bf16[128,512]{1,0:T(8,128)(2,1)S(1)} %get-tuple-element.33), channel_id=1, source_target_pairs={{1,0},{2,1},{3,2},{4,3},{5,4},{6,5},{7,6},{8,7},{9,8},{10,9},{11,1... | collective-permute-start | bytes 393224 | tf_op jit(solution)/shard_map/ppermute | solution.py:18
  562.9 5.5 copy-start.14
  577.1 2.5 copy-start.32
  577.2 2.5 copy-start.33
  588.7 3.4 copy-start.4
  592.1 2.5 copy-start.25
  592.1 2.5 copy-start.27
  592.1 2.5 copy-start.28
  594.6 3.1 copy-start.1
